TPU v7x, 32 devices: a whole 2x2x4 slice. The times are simulated.
32 devices in a mesh: row: 8 (over z, y), ma: 4 (over x, core).
Axes of the slice: x: 2, y: 2, z: 4, core: 2. Of those that a mesh axis runs over, the one named last changes fastest.
Arguments:
- thermal_state: float32 [64, 768, 2048], P('row', None, 'ma'), may hold values from -6 to 6
- sphere_node_annulus: int32 [64, 768], P('row'), may hold values from 0 to 1022, as said below
- sphere_node_offset: float32 [64, 768], P('row'), may hold values from 0 to 1
- integration_share: float32 [64, 768], P('row'), may hold values from 0.02 to 0.2
- annulus_holder_row: int32 [1024], replicated, may hold values from 0 to 7, never falling along the last dimension, each value on 1 to 256 neighbouring positions
- rotating_flow_potential: float32 [2048, 2048], P('row', 'ma'), may hold values from -6 to 6
Outputs:
- thermal_state_later: float32 [64, 768, 2048], P('row', None, 'ma')
- flow_potential_later: float32 [2048, 2048], P('row', 'ma')
Inputs may be any that keep to these rules, and one draw needn't show every extreme that they name: `sphere_node_annulus`: lower cell of each point; the next cell exists. `annulus_holder_row`: never falling along cells; each owner holds 1 to 256 cells and some owner exactly 256.
All inputs are finite; a program needn't handle non-finite values.
Results may differ from a plain program's by a relative error of at most 0.0003.
Values sent between devices are 32-bit elements; how exact they have to be, the bound alone decides.
A program may use at most 64 MiB of HBM per device.

v0:
```python
import math
import jax
import jax.numpy as jnp
from jax import lax
from jax.sharding import PartitionSpec as P

stream_step = 0.5
thermal_advance = 0.25


def extended(x, sides, width, wrap):
    for axis, dim in sides:
        size, length = (lax.axis_size(axis), x.shape[dim])
        up = [(i, (i + 1) % size) for i in range(size if wrap else size - 1)]
        down = [(j, i) for i, j in up]
        last = lax.slice_in_dim(x, length - width, length, axis=dim)
        leading = lax.slice_in_dim(x, 0, width, axis=dim)
        before = lax.ppermute(last, axis, up)
        after = lax.ppermute(leading, axis, down)
        x = jnp.concatenate([before, x, after], axis=dim)
    return x


def phi_diff(field):
    return (field[:, 2:] - field[:, :-2]) * 0.5


def qg_step(zint, stream, geo_slots):
    geo_column = geo_slots[:, None]
    extended_field = extended(jnp.stack([zint, stream]), (("ma", 2),), 2, True)
    forcing = -geo_column * phi_diff(extended_field[0])
    stream_wide = extended_field[1][:, 1:-1] + stream_step * forcing
    velocity = geo_column * phi_diff(stream_wide)
    return (stream_wide[:, 1:-1], velocity)


def per_device(
    thermal_state,
    sphere_node_annulus,
    sphere_node_offset,
    integration_share,
    annulus_holder_row,
    rotating_flow_potential,
):
    sphere_level_list, meridian_total, longitude_total = thermal_state.shape
    slot_most = rotating_flow_potential.shape[0]
    cell_count = annulus_holder_row.shape[0]
    cells = jnp.arange(cell_count, dtype=jnp.int32)
    before = jnp.sum(
        (annulus_holder_row[None, :] < annulus_holder_row[:, None]).astype(jnp.int32), axis=1
    )
    slot_of_cell = annulus_holder_row * slot_most + cells - before
    geo_cell = 1.0 / (0.25 + (cells.astype(jnp.float32) + 0.5) / cell_count)
    lower_cell = sphere_node_annulus.reshape(-1)
    slot_low = slot_of_cell[lower_cell]
    slot_high = slot_of_cell[lower_cell + 1]
    fraction = sphere_node_offset.reshape(-1)
    quadrature = integration_share.reshape(-1)
    below_share = quadrature * (1.0 - fraction)
    above_share = quadrature * fraction
    heat_vector_linear = thermal_state.reshape(-1, longitude_total)
    own_index = lax.axis_index("row")
    own_start = own_index * slot_most
    slot_rows = jnp.arange(lax.axis_size("row") * slot_most, dtype=jnp.int32)
    banded = jnp.where(slot_rows[:, None] == slot_low[None, :], below_share[None, :], 0.0)
    banded = banded + jnp.where(slot_rows[:, None] == slot_high[None, :], above_share[None, :], 0.0)
    zint = lax.psum_scatter(
        jnp.dot(
            banded,
            heat_vector_linear,
            precision=lax.Precision.HIGHEST,
            preferred_element_type=jnp.float32,
        ),
        "row",
        scatter_dimension=0,
        tiled=True,
    )
    slot_rows = own_start + jnp.arange(slot_most, dtype=jnp.int32)
    hits = slot_of_cell[None, :] == slot_rows[:, None]
    flow_potential_later, velocity = qg_step(
        zint, rotating_flow_potential, jnp.sum(jnp.where(hits, geo_cell[None, :], 0.0), axis=1)
    )
    piece = lax.all_gather(velocity, "row", axis=0, tiled=True)
    slot_cols = jnp.arange(piece.shape[0], dtype=jnp.int32)
    interp = jnp.where(slot_low[:, None] == slot_cols[None, :], (1.0 - fraction)[:, None], 0.0)
    interp = interp + jnp.where(slot_high[:, None] == slot_cols[None, :], fraction[:, None], 0.0)
    shifted_heat = jnp.dot(
        interp, piece, precision=lax.Precision.HIGHEST, preferred_element_type=jnp.float32
    )
    sphere_node_drift = shifted_heat.reshape(sphere_level_list, meridian_total, longitude_total)
    annulus_edges = extended(thermal_state, (("row", 0),), 1, False)
    distance_from_centre = (annulus_edges[2:] - annulus_edges[:-2]) * 0.5
    wrapped_heat_grid = jnp.pad(thermal_state, ((0, 0), (1, 1), (0, 0)))
    theta_from_north = (wrapped_heat_grid[:, 2:] - wrapped_heat_grid[:, :-2]) * 0.5
    angle = math.pi * (jnp.arange(meridian_total, dtype=jnp.float32) + 0.5) / meridian_total
    sin_theta_term = jnp.sin(angle)[None, :, None]
    cos_theta_term = jnp.cos(angle)[None, :, None]
    thermal_state_later = thermal_state - thermal_advance * sphere_node_drift * (
        sin_theta_term * distance_from_centre + cos_theta_term * theta_from_north
    )
    return (thermal_state_later, flow_potential_later)


def solution(mesh):
    return jax.shard_map(
        per_device,
        mesh=mesh,
        in_specs=(
            P("row", None, "ma"),
            P("row", None),
            P("row", None),
            P("row", None),
            P(),
            P("row", "ma"),
        ),
        out_specs=(P("row", None, "ma"), P("row", "ma")),
        check_vma=False,
    )
```

profile of v0, /device:TPU:0, one launch (start us, length us, event | category | flops | bytes accessed | tf_op | source)
XLA Modules:
  0.0 537.9 jit_solution(14528305836900812789)
XLA Ops:
  7.2 0.0 reduce-scatter.2.cloned.1.call-start
  7.2 1.3 convert_reduce_fusion
  8.5 0.7 add_subtract_fusion
  9.2 0.7 reshape.131
  10.0 0.8 copy.8
  10.7 0.7 reshape.132
  11.5 0.1 compare_select_fusion.1
  11.6 24.8 %gather_fusion = s32[6144]{0:T(1024)S(1)} fusion(s32[1024]{0:T(1024)S(1)} %add_subtract_fusion, s32[6144]{0:T(1024)S(1)} %broadcast_clamp_fusion.1), kind=kCustom, calls=%fused_computation | custom fusion | bytes 73728 | tf_op jit(solution)/shard_map/gather | solution.py:55
  36.3 24.8 %gather_fusion.1 = s32[6144]{0:T(1024)S(1)} fusion(s32[1024]{0:T(1024)S(1)} %add_subtract_fusion, s32[6144]{0:T(1024)S(1)} %broadcast_clamp_fusion), kind=kCustom, calls=%fused_computation.1 | custom fusion | bytes 73728 | tf_op jit(solution)/shard_map/gather | solution.py:56
  61.1 0.0 copy-start
  61.2 93.2 %fusion = f32[2048,512]{1,0:T(8,128)} fusion(f32[6144,512]{1,0:T(8,128)} %bitcast.18, f32[6144]{0:T(1024)S(1)} %get-tuple-element.11, s32[6144]{0:T(1024)S(1)} %gather_fusion.1, f32[6144]{0:T(1024)S(1)} %get-tuple-element.10, s32[6144]{0:T(1024)S(1)} %gather_fusion), kind=kOutput, calls=%fused_computation.2 | convolution fusion | flops 77372325888 | bytes 16875520 | tf_op jit(solution)/shard_map/dot_general | solution.py:68
  154.3 0.0 reduce-scatter.2.cloned.1.call-update
  154.4 0.0 all-gather.2.cloned.1.call-start
  154.4 0.2 select_reduce_fusion
  154.7 90.8 %reduce-scatter.2.cloned.1.call-done = f32[256,512]{1,0:T(8,128)} async-done(((f32[2048,512]{1,0:T(8,128)}), f32[256,512]{1,0:T(8,128)}) %reduce-scatter.2.cloned.1.call-update) | async-done | bytes 524304 | tf_op jit(solution)/shard_map/reduce_scatter | solution.py:67
  245.5 0.0 copy-done
  245.5 1.1 pad_maximum_fusion.4
  246.6 0.1 collective-permute-start
  246.7 1.7 collective-permute-start.1
  248.4 5.1 collective-permute-done
  253.5 0.8 collective-permute-done.1
  254.3 1.5 pad_maximum_fusion.2
  255.8 0.1 slice_bitcast_fusion.1
  255.9 0.5 fusion.28
  256.4 1.3 fusion.34
  257.7 0.0 all-gather.2.cloned.1.call-update
  257.7 3.8 fusion.33
  261.6 1.3 collective-permute-start.2
  262.9 4.6 collective-permute-start.3
  267.6 110.0 %all-gather.2.cloned.1.call-done = f32[2048,512]{1,0:T(8,128)} async-done(((f32[256,512]{1,0:T(8,128)}), f32[2048,512]{1,0:T(8,128)}) %all-gather.2.cloned.1.call-update) | async-done | bytes 4194320 | tf_op jit(solution)/shard_map/all_gather | solution.py:83
  377.6 123.0 %fusion.23 = f32[6144,512]{1,0:T(8,128)} fusion(f32[2048,512]{1,0:T(8,128)} %all-gather.2.cloned.1.call-done, f32[6144]{0:T(1024)S(1)} %reshape.131, s32[6144]{0:T(1024)S(1)} %gather_fusion.1, f32[6144]{0:T(1024)S(1)} %get-tuple-element.12, s32[6144]{0:T(1024)S(1)} %gather_fusion), kind=kOutput, calls=%fused_computation.31 | convolution fusion | flops 77375471616 | bytes 16875520 | tf_op jit(solution)/shard_map/dot_general | solution.py:87
  500.6 0.0 collective-permute-done.2
  500.6 0.0 collective-permute-done.3
  500.6 30.5 %fusion.22 = f32[8,768,512]{2,1,0:T(8,128)} fusion(f32[8,768,512]{2,1,0:T(8,128)} %param.6, f32[8,768,512]{2,1,0:T(8,128)} %bitcast.19, f32[1,768,512]{2,1,0:T(8,128)S(1)} %collective-permute-done.3, f32[1,768,512]{2,1,0:T(8,128)S(1)} %collective-permute-done.2, f32[768]{0:T(1024)S(1)} %get-tuple-element.17, f32[768]{0:T(1024)S(1)} %get-tuple-element.18), kind=kLoop, calls=%fused_computation.29 | loop fusion | flops 28311552 | bytes 40900608 | tf_op jit(solution)/shard_map/sub | solution.py:98
  (7 shorter events, 0.1 us)
Async XLA Ops:
  7.2 238.4 %reduce-scatter.2.cloned.1.call-start = ((), (), s32[]{:S(2)}) async-start(), calls=%async_computation.1 | async-start | bytes 4718592 | tf_op jit(solution)/shard_map/reduce_scatter | solution.py:67
  61.1 184.4 %copy-start = (f32[256,512]{1,0:T(8,128)S(1)}, f32[256,512]{1,0:T(8,128)}, u32[]{:S(2)}) copy-start(f32[256,512]{1,0:T(8,128)} %param.11) | copy-start | bytes 1572868
  154.4 223.2 %all-gather.2.cloned.1.call-start = ((), (), s32[]{:S(2)}) async-start(), calls=%async_computation.2 | async-start | bytes 4718592 | tf_op jit(solution)/shard_map/all_gather | solution.py:83
  246.6 6.9 %collective-permute-start = (f32[2,256,2]{2,1,0:T(8,128)S(1)}, f32[2,256,2]{2,1,0:T(8,128)S(1)}, u32[]{:S(2)}, u32[]{:S(2)}) collective-permute-start(f32[2,256,2]{2,1,0:T(8,128)S(1)} %get-tuple-element.6), channel_id=1, source_target_pairs={{0,1},{1,2},{2,3},{3,0},{4,5},{5,6},{6,7},{7,4},{8,9},{9,10},{10,1... | collective-permute-start | bytes 12296 | tf_op jit(solution)/shard_map/ppermute | solution.py:18
  246.7 7.6 %collective-permute-start.1 = (f32[2,256,2]{2,1,0:T(8,128)S(1)}, f32[2,256,2]{2,1,0:T(8,128)S(1)}, u32[]{:S(2)}, u32[]{:S(2)}) collective-permute-start(f32[2,256,2]{2,1,0:T(8,128)S(1)} %get-tuple-element.7), channel_id=1, source_target_pairs={{1,0},{2,1},{3,2},{0,3},{5,4},{6,5},{7,6},{4,7},{9,8},{10,9},{11,1... | collective-permute-start | bytes 12296 | tf_op jit(solution)/shard_map/ppermute | solution.py:19
  261.6 239.0 %collective-permute-start.2 = (f32[1,768,512]{2,1,0:T(8,128)}, f32[1,768,512]{2,1,0:T(8,128)S(1)}, u32[]{:S(2)}, u32[]{:S(2)}) collective-permute-start(f32[1,768,512]{2,1,0:T(8,128)} %get-tuple-element.2), channel_id=1, source_target_pairs={{4,0},{8,4},{12,8},{16,12},{20,16},{24,20},{28,24},{5,1},{9,5},{13... | collective-permute-start | bytes 4718600 | tf_op jit(solution)/shard_map/ppermute | solution.py:19
  262.9 237.7 %collective-permute-start.3 = (f32[1,768,512]{2,1,0:T(8,128)}, f32[1,768,512]{2,1,0:T(8,128)S(1)}, u32[]{:S(2)}, u32[]{:S(2)}) collective-permute-start(f32[1,768,512]{2,1,0:T(8,128)} %get-tuple-element.3), channel_id=1, source_target_pairs={{0,4},{4,8},{8,12},{12,16},{16,20},{20,24},{24,28},{1,5},{5,9},{9,... | collective-permute-start | bytes 4718600 | tf_op jit(solution)/shard_map/ppermute | solution.py:18
Sparse Core Ops, SparseCore 0:
  154.5 90.9 reduce-scatter.1
  257.9 119.6 all-gather.1
where the time goes:
time: 538 us
  matrix products  216 us (40%)
  waiting for transfers between devices  207 us (38%)
  local copies, waits for them, and re-layouts  55.7 us (10%)
  other arithmetic  37.3 us (7%)
  between operations  14.2 us (3%)
  starting transfers between devices  7.8 us (1%)
    dot_general x1, matrix products, per_device(): jnp.dot(interp, piece, precision=lax.Precision.HIGHEST, preferred_element...  123 us
    all_gather x1, waiting for transfers between devices, per_device(): piece = lax.all_gather(velocity, 'row', axis=0, tiled=True)  110 us
    dot_general x1, matrix products, per_device(): jnp.dot(banded, heat_vector_linear, precision=lax.Precision.HIGHEST, pref...  93.2 us
    reduce_scatter x1, waiting for transfers between devices, per_device(): lax.psum_scatter(jnp.dot(banded, heat_vector_linear, precision=lax.Precis...  90.8 us
    sub x1, other arithmetic, per_device(): thermal_state - thermal_advance * sphere_node_drift * (sin_theta_term * d...  30.5 us
    gather x1, local copies, waits for them, and re-layouts, per_device(): slot_low = slot_of_cell[lower_cell]  24.8 us
    gather x1, local copies, waits for them, and re-layouts, per_device(): slot_high = slot_of_cell[lower_cell + 1]  24.8 us
  transfers between devices with their start and end apart: 6, of which 4 were waited for; matrix products, arithmetic and copies ran while one was open for 24% of the time, Pallas kernels for 0%

commit v1 on v0

--- a/solution.py
+++ b/solution.py
@@ -80,7 +80,10 @@
     flow_potential_later, velocity = qg_step(
         zint, rotating_flow_potential, jnp.sum(jnp.where(hits, geo_cell[None, :], 0.0), axis=1)
     )
-    piece = lax.all_gather(velocity, "row", axis=0, tiled=True)
+    answer = tuple((velocity for _ in range(lax.psum(1, "row"))))
+    y = jnp.stack(answer)
+    next_value = lax.all_to_all(y, "row", 0, 0)
+    piece = jnp.concatenate(next_value, axis=0)
     slot_cols = jnp.arange(piece.shape[0], dtype=jnp.int32)
     interp = jnp.where(slot_low[:, None] == slot_cols[None, :], (1.0 - fraction)[:, None], 0.0)
     interp = interp + jnp.where(slot_high[:, None] == slot_cols[None, :], fraction[:, None], 0.0)

time: 538 us -> 514 us (0.955)
  the two profiles are of different devices: /device:TPU:0 before, /device:TPU:13 now
where the time goes in v1:
time: 514 us
  waiting for transfers between devices  214 us (42%)
  matrix products  209 us (41%)
  local copies, waits for them, and re-layouts  56.6 us (11%)
  between operations  14.2 us (3%)
  starting transfers between devices  12.9 us (3%)
  other arithmetic  6.62 us (1%)
    ppermute x2, waiting for transfers between devices, extended(): after = lax.ppermute(leading, axis, down)  119 us
    dot_general x1, matrix products, per_device(): jnp.dot(interp, piece, precision=lax.Precision.HIGHEST, preferred_element...  116 us
    dot_general x1, matrix products, per_device(): jnp.dot(banded, heat_vector_linear, precision=lax.Precision.HIGHEST, pref...  93.2 us
    reduce_scatter x1, waiting for transfers between devices, per_device(): lax.psum_scatter(jnp.dot(banded, heat_vector_linear, precision=lax.Precis...  89.1 us
    gather x1, local copies, waits for them, and re-layouts, per_device(): slot_low = slot_of_cell[lower_cell]  24.8 us
    gather x1, local copies, waits for them, and re-layouts, per_device(): slot_high = slot_of_cell[lower_cell + 1]  24.8 us
  transfers between devices with their start and end apart: 6, of which 4 were waited for; matrix products, arithmetic and copies ran while one was open for 0% of the time, Pallas kernels for 0%

profile of v1, /device:TPU:13, one launch (start us, length us, event | category | flops | bytes accessed | tf_op | source)
XLA Modules:
  0.0 513.5 jit_solution(8957935394605597259)
XLA Ops:
  7.2 0.0 reduce-scatter.2.cloned.1.call-start
  7.2 1.3 convert_reduce_fusion
  8.5 0.7 add_subtract_fusion
  9.2 0.8 copy.8
  10.0 0.7 reshape.193
  10.7 0.7 reshape.194
  11.5 0.1 compare_select_fusion.1
  11.6 24.8 %gather_fusion = s32[6144]{0:T(1024)S(1)} fusion(s32[1024]{0:T(1024)S(1)} %add_subtract_fusion, s32[6144]{0:T(1024)S(1)} %broadcast_clamp_fusion.1), kind=kCustom, calls=%fused_computation | custom fusion | bytes 73728 | tf_op jit(solution)/shard_map/gather | solution.py:55
  36.3 24.8 %gather_fusion.1 = s32[6144]{0:T(1024)S(1)} fusion(s32[1024]{0:T(1024)S(1)} %add_subtract_fusion, s32[6144]{0:T(1024)S(1)} %broadcast_clamp_fusion), kind=kCustom, calls=%fused_computation.1 | custom fusion | bytes 73728 | tf_op jit(solution)/shard_map/gather | solution.py:56
  61.1 0.0 copy-start
  61.2 93.2 %fusion.2 = f32[2048,512]{1,0:T(8,128)} fusion(f32[6144,512]{1,0:T(8,128)} %bitcast.31, f32[6144]{0:T(1024)S(1)} %get-tuple-element.11, s32[6144]{0:T(1024)S(1)} %gather_fusion.1, f32[6144]{0:T(1024)S(1)} %get-tuple-element.10, s32[6144]{0:T(1024)S(1)} %gather_fusion), kind=kOutput, calls=%fused_computation.4 | convolution fusion | flops 77372325888 | bytes 16875520 | tf_op jit(solution)/shard_map/dot_general | solution.py:68
  154.3 0.0 reduce-scatter.2.cloned.1.call-update
  154.4 0.2 select_reduce_fusion
  154.6 89.1 %reduce-scatter.2.cloned.1.call-done = f32[256,512]{1,0:T(8,128)} async-done(((f32[2048,512]{1,0:T(8,128)}), f32[256,512]{1,0:T(8,128)}) %reduce-scatter.2.cloned.1.call-update) | async-done | bytes 524304 | tf_op jit(solution)/shard_map/reduce_scatter | solution.py:67
  243.7 0.0 copy-done
  243.7 1.1 pad_maximum_fusion.4
  244.9 2.2 collective-permute-start
  247.1 0.0 collective-permute-start.1
  247.1 5.3 %collective-permute-done = f32[2,256,2]{2,1,0:T(8,128)S(1)} collective-permute-done((f32[2,256,2]{2,1,0:T(8,128)S(1)}, f32[2,256,2]{2,1,0:T(8,128)S(1)}, u32[]{:S(2)}, u32[]{:S(2)}) %collective-permute-start) | collective-permute-done | bytes 4128 | tf_op jit(solution)/shard_map/ppermute | solution.py:18
  252.3 1.6 collective-permute-done.1
  253.9 1.5 pad_maximum_fusion.2
  255.4 0.1 slice_bitcast_fusion.1
  255.5 0.0 copy-start.1
  255.5 0.4 fusion.28
  256.0 1.2 fusion.33
  257.2 2.5 stack.11
  259.7 4.5 all-to-all-start
  264.2 2.2 fusion.32
  266.4 2.2 collective-permute-start.2
  268.6 4.0 collective-permute-start.3
  272.7 0.0 copy-done.1
  272.7 117.9 %collective-permute-done.2 = f32[1,768,512]{2,1,0:T(8,128)} collective-permute-done((f32[1,768,512]{2,1,0:T(8,128)S(1)}, f32[1,768,512]{2,1,0:T(8,128)}, u32[]{:S(2)}, u32[]{:S(2)}) %collective-permute-start.2) | collective-permute-done | bytes 1572896 | tf_op jit(solution)/shard_map/ppermute | solution.py:19
  390.6 0.0 collective-permute-done.3
  390.6 0.0 all-to-all-done
  390.6 116.0 %fusion.23 = f32[8,768,512]{2,1,0:T(8,128)} fusion(f32[8,768,512]{2,1,0:T(8,128)} %param.6, f32[1,768,512]{2,1,0:T(8,128)} %collective-permute-done.3, f32[1,768,512]{2,1,0:T(8,128)} %collective-permute-done.2, f32[768]{0:T(1024)S(1)} %get-tuple-element.16, f32[768]{0:T(1024)S(1)} %get-tuple-element.17, f32[2048,512,1]{1,0,2:T(8,128)} %bitcast.9, ...), kind=kOutput, calls=%fused_computation.30 | convolution fusion | flops 77403783168 | bytes 32610304 | tf_op jit(solution)/shard_map/dot_general | solution.py:90
  (10 shorter events, 0.1 us)
Async XLA Ops:
  7.2 236.6 %reduce-scatter.2.cloned.1.call-start = ((), (), s32[]{:S(2)}) async-start(), calls=%async_computation.2 | async-start | bytes 4718592 | tf_op jit(solution)/shard_map/reduce_scatter | solution.py:67
  61.1 182.6 %copy-start = (f32[256,512]{1,0:T(8,128)S(1)}, f32[256,512]{1,0:T(8,128)}, u32[]{:S(2)}) copy-start(f32[256,512]{1,0:T(8,128)} %param.11) | copy-start | bytes 1572868
  244.9 7.5 %collective-permute-start = (f32[2,256,2]{2,1,0:T(8,128)S(1)}, f32[2,256,2]{2,1,0:T(8,128)S(1)}, u32[]{:S(2)}, u32[]{:S(2)}) collective-permute-start(f32[2,256,2]{2,1,0:T(8,128)S(1)} %get-tuple-element.6), channel_id=1, source_target_pairs={{0,1},{1,2},{2,3},{3,0},{4,5},{5,6},{6,7},{7,4},{8,9},{9,10},{10,1... | collective-permute-start | bytes 12296 | tf_op jit(solution)/shard_map/ppermute | solution.py:18
  247.1 6.8 %collective-permute-start.1 = (f32[2,256,2]{2,1,0:T(8,128)S(1)}, f32[2,256,2]{2,1,0:T(8,128)S(1)}, u32[]{:S(2)}, u32[]{:S(2)}) collective-permute-start(f32[2,256,2]{2,1,0:T(8,128)S(1)} %get-tuple-element.7), channel_id=1, source_target_pairs={{1,0},{2,1},{3,2},{0,3},{5,4},{6,5},{7,6},{4,7},{9,8},{10,9},{11,1... | collective-permute-start | bytes 12296 | tf_op jit(solution)/shard_map/ppermute | solution.py:19
  255.5 17.2 %copy-start.1 = (f32[8,768]{1,0:T(8,128)S(1)}, f32[8,768]{1,0:T(8,128)}, u32[]{:S(2)}) copy-start(f32[8,768]{1,0:T(8,128)} %param.8) | copy-start | bytes 73732
  259.7 130.9 %all-to-all-start = ((f32[8,256,512]{2,1,0:T(8,128)}), f32[8,256,512]{2,1,0:T(8,128)}, u32[]{:S(2)}, u32[]{:S(2)}) async-start(f32[8,256,512]{2,1,0:T(8,128)} %stack.11), calls=%async_computation.1 | async-start | bytes 8388608 | tf_op jit(solution)/shard_map/all_to_all | solution.py:85
  266.4 124.2 %collective-permute-start.2 = (f32[1,768,512]{2,1,0:T(8,128)S(1)}, f32[1,768,512]{2,1,0:T(8,128)}, u32[]{:S(2)}, u32[]{:S(2)}) collective-permute-start(f32[1,768,512]{2,1,0:T(8,128)S(1)} %get-tuple-element.2), channel_id=1, source_target_pairs={{4,0},{8,4},{12,8},{16,12},{20,16},{24,20},{28,24},{5,1},{9,5},{13... | collective-permute-start | bytes 4718600 | tf_op jit(solution)/shard_map/ppermute | solution.py:19
  268.6 122.0 %collective-permute-start.3 = (f32[1,768,512]{2,1,0:T(8,128)S(1)}, f32[1,768,512]{2,1,0:T(8,128)}, u32[]{:S(2)}, u32[]{:S(2)}) collective-permute-start(f32[1,768,512]{2,1,0:T(8,128)S(1)} %get-tuple-element.3), channel_id=1, source_target_pairs={{0,4},{4,8},{8,12},{12,16},{16,20},{20,24},{24,28},{1,5},{5,9},{9,... | collective-permute-start | bytes 4718600 | tf_op jit(solution)/shard_map/ppermute | solution.py:18
Sparse Core Ops, SparseCore 0:
  154.5 89.2 reduce-scatter.1
